TPU v7x, 32 devices: a whole 2x2x4 slice. The times are simulated.
32 devices in a mesh: freq: 4 (over y, x), shot: 8 (over z, core).
Axes of the slice: x: 2, y: 2, z: 4, core: 2. Of those that a mesh axis runs over, the one named last changes fastest.
Arguments:
- traces: bfloat16 [2, 4, 3072, 3072], P(None, 'freq', 'shot'), may hold values from -40 to 40, as said below
Outputs:
- multiples: bfloat16 [2, 4, 3072, 3072], P(None, 'freq', 'shot')
- primaries: bfloat16 [2, 4, 3072, 3072], P(None, 'freq', 'shot')
Inputs may be any that keep to these rules, and one draw needn't show every extreme that they name: `traces`: finite recorded data.
All inputs are finite; a program needn't handle non-finite values.
Results may differ from a plain program's by a relative error of at most 0.0005.
Values may be sent and summed in bfloat16 or wider, within the bound.
A program may use at most 192 MiB of HBM per device.

v0:
```python
import functools
import math

import jax
import jax.numpy as jnp
from jax import lax
from jax.experimental import pallas as pl
from jax.experimental.pallas import tpu as pltpu
from jax.sharding import PartitionSpec as P

epsilon = 1e-06
MESH = pl.DeviceIdType.MESH


def complex_product(left_re, left_im, right):
    left_block = jnp.stack(
        [jnp.concatenate([left_re, -left_im], axis=2), jnp.concatenate([left_im, left_re], axis=2)]
    )
    right_block = jnp.concatenate([right[0], right[1]], axis=1)
    return jnp.einsum("cfik,fkn->cfin", left_block, right_block, preferred_element_type=jnp.float32)


def finish(traces, mult_re, mult_im, num_re, num_im, denom):
    matrix_order = traces.shape[3]
    data_re = traces[0].astype(jnp.float32)
    data_im = traces[1].astype(jnp.float32)
    total_count = float(traces.shape[1] * lax.axis_size("freq") * matrix_order * matrix_order)
    scaled_den = denom / total_count + epsilon
    fit_re = num_re / total_count / scaled_den
    fit_im = num_im / total_count / scaled_den
    prim_re = data_re - (fit_re * mult_re - fit_im * mult_im)
    prim_im = data_im - (fit_re * mult_im + fit_im * mult_re)
    multiples = jnp.stack([mult_re, mult_im]).astype(jnp.bfloat16)
    primaries = jnp.stack([prim_re, prim_im]).astype(jnp.bfloat16)
    return (multiples, primaries)


def gathered(traces):
    factor = 1.0 / math.sqrt(traces.shape[3])
    products = complex_product(
        traces[0], traces[1], lax.all_gather(traces, "shot", axis=2, tiled=True)
    )
    mult_re = products[0] * factor
    mult_im = products[1] * factor
    data_re = traces[0].astype(jnp.float32)
    data_im = traces[1].astype(jnp.float32)
    sums = lax.psum(
        jnp.stack([
            jnp.sum(mult_re * data_re + mult_im * data_im),
            jnp.sum(mult_re * data_im - mult_im * data_re),
            jnp.sum(mult_re * mult_re + mult_im * mult_im),
        ]),
        ("freq", "shot"),
    )
    return finish(traces, mult_re, mult_im, sums[0], sums[1], sums[2])


def line_kernel(
    chunks, kept, width, step, freqs, shots,
    traces_ref, mult_ref, total_ref,
    grid, help_stage, acc, sums,
    load_sem, ici_recv, pair_recv, far_send, end_send, pair_send,
    result_send, result_recv, sum_send, sum_recv,
):
    rows = traces_ref.shape[2]
    order = traces_ref.shape[3]
    factor = 1.0 / math.sqrt(order)
    freq = lax.axis_index("freq")
    shot = lax.axis_index("shot")
    z = shot // 2
    core = shot % 2
    low = z < 2
    end = jnp.where(low, 0, 3)
    mid = jnp.where(low, 1, 2)
    far_mid = jnp.where(low, 2, 1)
    far_end = jnp.where(low, 3, 0)
    is_end = z == end

    def block(chip, plane, j):
        first = pl.multiple_of((chip * 2 + plane) * rows, rows)
        return grid.at[:, pl.ds(first, rows), pl.ds(pl.multiple_of(j * width, width), width)]

    def remote(src, dst, send, recv, chip, plane):
        return pltpu.make_async_remote_copy(
            src_ref=src, dst_ref=dst, send_sem=send, recv_sem=recv,
            device_id=(freq, chip * 2 + plane), device_id_type=MESH,
        )

    def ici(chip, j, send, slot, target):
        ref = block(chip, core, j)
        return remote(ref, ref, send, ici_recv.at[slot, j], target, core)

    def pair(chip, j, slot):
        ref = block(chip, core, j)
        return remote(ref, ref, pair_send.at[slot, j], pair_recv.at[slot, j], z, 1 - core)

    def arrived(chip, j, slot):
        ref = block(chip, core, j)
        remote(ref, ref, far_send.at[0, j], ici_recv.at[slot, j], z, 1 - core).wait_recv()

    def paired(chip, j, slot):
        ref = block(chip, 1 - core, j)
        remote(ref, ref, pair_send.at[slot, j], pair_recv.at[slot, j], z, 1 - core).wait_recv()

    def to_end(chip, j, slot):
        return ici(chip, j, end_send.at[slot, j], slot, end)

    def to_far(chip, j, slot):
        return ici(chip, j, far_send.at[slot, j], slot + 1, far_mid)

    def to_mid(j):
        return ici(z, j, end_send.at[0, j], 0, mid)

    def result(j, s):
        return remote(
            help_stage.at[s],
            mult_ref.at[:, :, pl.ds(pl.multiple_of(j * width, width), width)],
            result_send.at[s], result_recv.at[j], end, core,
        )

    def multiply(chip, j, stage, start):
        first = pl.multiple_of((chip * 2 + core) * rows, rows)

        def part(q, carry):
            column = pl.multiple_of(j * width + q * step, step)
            left_re = grid[0, pl.ds(first, rows), :]
            left_im = grid[1, pl.ds(first, rows), :]
            right_re = grid[0, :, pl.ds(column, step)]
            right_im = grid[1, :, pl.ds(column, step)]
            dot = functools.partial(jnp.dot, preferred_element_type=jnp.float32)
            mult_re = (dot(left_re, right_re) - dot(left_im, right_im)) * factor
            mult_im = (dot(left_re, right_im) + dot(left_im, right_re)) * factor
            here = pl.ds(pl.multiple_of(start + q * step, step), step)
            stage[0, :, here] = mult_re
            stage[1, :, here] = mult_im
            data_re = grid[0, pl.ds(first, rows), pl.ds(column, step)].astype(jnp.float32)
            data_im = grid[1, pl.ds(first, rows), pl.ds(column, step)].astype(jnp.float32)
            for i, term in enumerate((
                mult_re * data_re + mult_im * data_im,
                mult_re * data_im - mult_im * data_re,
                mult_re * mult_re + mult_im * mult_im,
            )):
                folded = jnp.sum(term.reshape(rows // 8, 8, step), axis=0)
                lanes = folded[:, :128]
                for k in range(1, step // 128):
                    lanes = lanes + folded[:, k * 128:(k + 1) * 128]
                acc[pl.ds(i * 8, 8), :] += lanes
            return carry

        lax.fori_loop(0, width // step, part, 0)

    acc[...] = jnp.zeros_like(acc)
    mine = grid.at[:, pl.ds(pl.multiple_of(shot * rows, rows), rows), :]
    load = pltpu.make_async_copy(traces_ref.at[:, 0], mine, load_sem)
    load.start()
    load.wait()

    def loop(lower, upper, body):
        def run(j, carry):
            body(j)
            return carry
        lax.fori_loop(lower, upper, run, 0)

    @pl.when(is_end)
    def _():
        def first_sends(j):
            to_mid(j).start()

            @pl.when(j < kept)
            def _():
                pair(z, j, 3).start()

        loop(0, chunks, first_sends)

        def work(j):
            for slot, chip in enumerate((mid, far_mid, far_end)):
                arrived(chip, j, slot)
                pair(chip, j, slot).start()
            for slot, chip in enumerate((mid, far_mid, far_end, end)):
                paired(chip, j, slot)
            multiply(z, j, mult_ref, j * width)

        loop(0, kept, work)

        def drain(j):
            to_mid(j).wait_send()

            @pl.when(j < kept)
            def _():
                for slot, chip in enumerate((mid, far_mid, far_end, end)):
                    pair(chip, j, slot).wait_send()

        loop(0, chunks, drain)

    @pl.when(jnp.logical_not(is_end))
    def _():
        def own_sends(j):
            to_far(z, j, 0).start()

            @pl.when(j < kept)
            def _():
                to_end(z, j, 0).start()
            pair(z, j, 3).start()

        def near(j):
            arrived(end, j, 0)
            to_far(end, j, 1).start()
            pair(end, j, 0).start()

        ahead = 2
        loop(0, ahead, own_sends)
        loop(0, ahead, near)

        def work(j):
            for slot, chip in ((1, far_mid), (2, far_end)):
                arrived(chip, j, slot)

                @pl.when(j < kept)
                def _():
                    to_end(chip, j, slot).start()
                pair(chip, j, slot).start()
            for slot, chip in ((1, far_mid), (2, far_end), (3, z)):
                paired(chip, j, slot)
            upper = jnp.where(j < kept, jnp.minimum(j + ahead + 1, chunks), chunks)
            lower = jnp.where(j <= kept, jnp.minimum(j + ahead, chunks), chunks)

            def more(jj):
                own_sends(jj)
                near(jj)

            loop(lower, upper, more)
            paired(end, j, 0)
            s = j % 2

            @pl.when(j >= kept)
            def _():
                @pl.when(j >= kept + 2)
                def _():
                    result(j - 2, s).wait_send()
                multiply(end, j, help_stage.at[s], 0)
                result(j, s).start()

            multiply(z, j, mult_ref, j * width)

        loop(0, chunks, work)

        def drain(j):
            to_far(z, j, 0).wait_send()
            to_far(end, j, 1).wait_send()
            for slot, chip in enumerate((end, far_mid, far_end, z)):
                pair(chip, j, slot).wait_send()

            @pl.when(j < kept)
            def _():
                for slot, chip in enumerate((z, far_mid, far_end)):
                    to_end(chip, j, slot).wait_send()

        loop(0, chunks, drain)

    devices = freqs * shots
    me = freq * shots + shot

    def give(d):
        target = (me + d) % devices
        return pltpu.make_async_remote_copy(
            src_ref=acc, dst_ref=sums.at[d - 1],
            send_sem=sum_send.at[d - 1], recv_sem=sum_recv.at[d - 1],
            device_id=(target // shots, target % shots), device_id_type=MESH,
        )

    loop(1, devices, lambda d: give(d).start())
    loop(1, devices, lambda d: give(d).wait_recv())
    total_ref[...] = acc[...] + jnp.sum(sums[...], axis=0)

    @pl.when(is_end)
    def _():
        loop(kept, chunks, lambda j: result(j, 0).wait_recv())

    @pl.when(jnp.logical_not(is_end))
    def _():
        def last(j):
            result(j, j % 2).wait_send()
        loop(chunks - 2, chunks, last)

    loop(1, devices, lambda d: give(d).wait_send())


def epilogue_kernel(total_count, total_ref, traces_ref, mult_ref, multiples_ref, primaries_ref, fit):
    @pl.when(pl.program_id(0) == 0)
    def _():
        num_re, num_im, denom = (jnp.sum(total_ref[pl.ds(8 * i, 8), :]) for i in range(3))
        scaled_den = denom / total_count + epsilon
        fit[0] = num_re / total_count / scaled_den
        fit[1] = num_im / total_count / scaled_den

    fit_re = fit[0]
    fit_im = fit[1]
    strip = traces_ref.shape[2]
    first = pl.multiple_of(pl.program_id(0) * strip, strip)
    mult_re = mult_ref[0, pl.ds(first, strip), :]
    mult_im = mult_ref[1, pl.ds(first, strip), :]
    data_re = traces_ref[0, 0].astype(jnp.float32)
    data_im = traces_ref[1, 0].astype(jnp.float32)
    prim_re = data_re - (fit_re * mult_re - fit_im * mult_im)
    prim_im = data_im - (fit_re * mult_im + fit_im * mult_re)
    multiples_ref[0, 0] = mult_re.astype(jnp.bfloat16)
    multiples_ref[1, 0] = mult_im.astype(jnp.bfloat16)
    primaries_ref[0, 0] = prim_re.astype(jnp.bfloat16)
    primaries_ref[1, 0] = prim_im.astype(jnp.bfloat16)


def on_a_line(traces):
    rows, order = traces.shape[2], traces.shape[3]
    freqs, shots = lax.axis_size("freq"), lax.axis_size("shot")
    step = 256
    width = step
    chunks = order // width
    kept = chunks // 3
    devices = freqs * shots
    dma = pltpu.SemaphoreType.DMA
    mult, totals = pl.pallas_call(
        functools.partial(line_kernel, chunks, kept, width, step, freqs, shots),
        out_shape=(
            pltpu.VMEM((2, rows, order), jnp.float32),
            jax.ShapeDtypeStruct((24, 128), jnp.float32),
        ),
        in_specs=[pl.BlockSpec(memory_space=pltpu.HBM)],
        out_specs=(
            pl.BlockSpec(memory_space=pltpu.VMEM),
            pl.BlockSpec(memory_space=pltpu.VMEM),
        ),
        scratch_shapes=[
            pltpu.VMEM((2, order, order), jnp.bfloat16),
            pltpu.VMEM((2, 2, rows, width), jnp.float32),
            pltpu.VMEM((24, 128), jnp.float32),
            pltpu.VMEM((devices - 1, 24, 128), jnp.float32),
            dma, dma((3, chunks)), dma((4, chunks)), dma((2, chunks)),
            dma((3, chunks)), dma((4, chunks)),
            dma((2,)), dma((chunks,)), dma((devices - 1,)), dma((devices - 1,)),
        ],
        compiler_params=pltpu.CompilerParams(
            has_side_effects=True, vmem_limit_bytes=48 * 1024 * 1024
        ),
    )(traces)
    strip = rows // 12 if rows % (12 * 16) == 0 else rows
    block = pl.BlockSpec((2, 1, strip, order), lambda i: (0, 0, i, 0))
    out = jax.ShapeDtypeStruct(traces.shape, traces.dtype)
    return pl.pallas_call(
        functools.partial(epilogue_kernel, float(freqs * order * order)),
        grid=(rows // strip,),
        out_shape=(out, out),
        in_specs=[
            pl.BlockSpec((24, 128), lambda i: (0, 0)),
            block,
            pl.BlockSpec(memory_space=pltpu.VMEM),
        ],
        out_specs=(block, block),
        scratch_shapes=[pltpu.SMEM((2,), jnp.float32)],
        compiler_params=pltpu.CompilerParams(
            dimension_semantics=("arbitrary",), vmem_limit_bytes=24 * 1024 * 1024
        ),
    )(totals, traces, mult)


def solution(mesh):
    placed = P(None, "freq", "shot", None)

    def per_device(traces):
        four_chips = mesh.shape["shot"] == 2 * 4
        if four_chips and traces.shape[1] == 1 and traces.shape[3] % 256 == 0:
            return on_a_line(traces)
        return gathered(traces)

    return jax.shard_map(
        per_device, mesh=mesh, in_specs=(placed,), out_specs=(placed, placed), check_vma=False
    )
```

profile of v0, /device:TPU:1, one launch (start us, length us, event | category | flops | bytes accessed | tf_op | source)
XLA Modules:
  0.0 270.7 jit_solution(16265873779322499492)
XLA Ops:
  0.6 0.0 copy-start
  0.6 262.2 %shard_map.30 = (f32[2,384,3072]{2,1,0:T(8,128)S(1)}, f32[24,128]{1,0:T(8,128)}) custom-call(bf16[2,1,384,3072]{3,2,1,0:T(8,128)(2,1)} %traces_ref.3), custom_call_target="tpu_custom_call" | custom-call | tf_op jit(solution)/shard_map/pallas_call | solution.py:321
  262.8 0.0 copy-done
  262.8 0.0 copy-start.1
  262.8 0.7 copy-done.1
  263.5 7.2 %shard_map.31 = (bf16[2,1,384,3072]{3,2,1,0:T(8,128)(2,1)}, bf16[2,1,384,3072]{3,2,1,0:T(8,128)(2,1)}) custom-call(f32[24,128]{1,0:T(8,128)S(1)} %copy-done.1, bf16[2,1,384,3072]{3,2,1,0:T(8,128)(2,1)S(1)} %copy-done, f32[2,384,3072]{2,1,0:T(8,128)S(1)} %get-tuple-element.5.mult_ref), custom_call_target="tpu_custom_call" | custom-call | tf_op jit(solution)/shard_map/pallas_call | solution.py:348
Async XLA Ops:
  0.6 262.2 %copy-start = (bf16[2,1,384,3072]{3,2,1,0:T(8,128)(2,1)S(1)}, bf16[2,1,384,3072]{3,2,1,0:T(8,128)(2,1)}, u32[]{:S(2)}) copy-start(bf16[2,1,384,3072]{3,2,1,0:T(8,128)(2,1)} %traces_ref.3) | copy-start | bytes 14155780
  262.8 0.7 copy-start.1
where the time goes:
time: 271 us
  Pallas kernels  269 us (99%)
    pallas_call x1, Pallas kernels, on_a_line(): pl.pallas_call(functools.partial(line_kernel, chunks, kept, width, step,...  262 us
    pallas_call x1, Pallas kernels, on_a_line(): pl.pallas_call(functools.partial(epilogue_kernel, float(freqs * order * o...  7.18 us

commit v1 on v0

v1 whole, which is shorter than its diff:
```python
import functools
import math

import jax
import jax.numpy as jnp
from jax import lax
from jax.experimental import pallas as pl
from jax.experimental.pallas import tpu as pltpu
from jax.sharding import PartitionSpec as P

epsilon = 1e-06
MESH = pl.DeviceIdType.MESH
LANES = 128


def complex_product(left_re, left_im, right):
    left_block = jnp.stack(
        [jnp.concatenate([left_re, -left_im], axis=2), jnp.concatenate([left_im, left_re], axis=2)]
    )
    right_block = jnp.concatenate([right[0], right[1]], axis=1)
    return jnp.einsum("cfik,fkn->cfin", left_block, right_block, preferred_element_type=jnp.float32)


def finish(traces, mult_re, mult_im, num_re, num_im, denom):
    matrix_order = traces.shape[3]
    data_re = traces[0].astype(jnp.float32)
    data_im = traces[1].astype(jnp.float32)
    total_count = float(traces.shape[1] * lax.axis_size("freq") * matrix_order * matrix_order)
    scaled_den = denom / total_count + epsilon
    fit_re = num_re / total_count / scaled_den
    fit_im = num_im / total_count / scaled_den
    prim_re = data_re - (fit_re * mult_re - fit_im * mult_im)
    prim_im = data_im - (fit_re * mult_im + fit_im * mult_re)
    multiples = jnp.stack([mult_re, mult_im]).astype(jnp.bfloat16)
    primaries = jnp.stack([prim_re, prim_im]).astype(jnp.bfloat16)
    return (multiples, primaries)


def gathered(traces):
    factor = 1.0 / math.sqrt(traces.shape[3])
    products = complex_product(
        traces[0], traces[1], lax.all_gather(traces, "shot", axis=2, tiled=True)
    )
    mult_re = products[0] * factor
    mult_im = products[1] * factor
    data_re = traces[0].astype(jnp.float32)
    data_im = traces[1].astype(jnp.float32)
    sums = lax.psum(
        jnp.stack([
            jnp.sum(mult_re * data_re + mult_im * data_im),
            jnp.sum(mult_re * data_im - mult_im * data_re),
            jnp.sum(mult_re * mult_re + mult_im * mult_im),
        ]),
        ("freq", "shot"),
    )
    return finish(traces, mult_re, mult_im, sums[0], sums[1], sums[2])


def end_schedule(chunks, groups, ready):
    done = [0] * chunks
    pieces = []

    def column(c):
        if done[c] < groups:
            pieces.append((done[c], groups - done[c], c, 1))
            left = groups - done[c]
            done[c] = groups
            return left
        return 0

    window = 2 * groups
    room = window - column(0) - column(1)
    following = 2
    while min(done) < groups:
        while room > 0 and min(done) < groups:
            group = min(done)
            first = done.index(group)
            last = first
            while last < chunks and done[last] == group and last - first < room:
                last += 1
            pieces.append((group, 1, first, last - first))
            done[first:last] = [group + 1] * (last - first)
            room -= last - first
        room += window
        if following < chunks:
            room -= column(following)
            following += 1
    out = []
    for group, count, first, width in pieces:
        column_need = first - 2
        group_need = min(ready[g] for g in range(group, group + count))
        out.append((group, count, first, width, max(-1, min(column_need, group_need))))
    return tuple(out)


def line_kernel(
    chunks, kept, groups, ready, schedule, freqs,
    traces_ref, mult_ref, total_ref,
    grid, stage, acc, packed, partial_in,
    load_sem, piece_send, piece_recv, ici_recv, far_send, end_send, pair_send, pair_recv,
    result_send, result_recv, sum_send, sum_recv,
):
    rows = traces_ref.shape[2]
    order = traces_ref.shape[3]
    group_rows = rows // groups
    factor = 1.0 / math.sqrt(order)
    freq = lax.axis_index("freq")
    shot = lax.axis_index("shot")
    z = shot // 2
    core = shot % 2
    low = z < 2
    end = jnp.where(low, 0, 3)
    mid = jnp.where(low, 1, 2)
    far_mid = jnp.where(low, 2, 1)
    far_end = jnp.where(low, 3, 0)
    is_end = z == end
    beside = freq + 1 - 2 * (freq % 2)
    across = (freq + 2) % freqs

    def row(chip, plane):
        return pl.multiple_of((chip * 2 + plane) * rows, rows)

    def lane(j):
        return pl.multiple_of(j * LANES, LANES)

    def block(chip, plane, j):
        return grid.at[:, pl.ds(row(chip, plane), rows), pl.ds(lane(j), LANES)]

    def remote(src, dst, send, recv, chip, plane):
        return pltpu.make_async_remote_copy(
            src_ref=src, dst_ref=dst, send_sem=send, recv_sem=recv,
            device_id=(freq, chip * 2 + plane), device_id_type=MESH,
        )

    def ici(chip, j, send, slot, target):
        ref = block(chip, core, j)
        return remote(ref, ref, send, ici_recv.at[slot, j], target, core)

    def pair(chip, j, slot):
        ref = block(chip, core, j)
        return remote(ref, ref, pair_send.at[slot, j], pair_recv.at[slot, j], z, 1 - core)

    def arrived(chip, j, slot):
        ref = block(chip, core, j)
        remote(ref, ref, far_send.at[0, j], ici_recv.at[slot, j], z, 1 - core).wait_recv()

    def paired(chip, j, slot):
        ref = block(chip, 1 - core, j)
        remote(ref, ref, pair_send.at[slot, j], pair_recv.at[slot, j], z, 1 - core).wait_recv()

    def to_end(chip, j, slot):
        return ici(chip, j, end_send.at[slot, j], slot, end)

    def to_far(chip, j, slot):
        return ici(chip, j, far_send.at[slot, j], slot + 1, far_mid)

    def piece(d):
        group, count, first, width, _ = schedule[d]
        ref = grid.at[
            :,
            pl.ds(pl.multiple_of(row(end, core) + group * group_rows, group_rows), count * group_rows),
            pl.ds(first * LANES, width * LANES),
        ]
        return remote(ref, ref, piece_send.at[d], piece_recv.at[d], mid, core)

    def result(g, j):
        here = pl.ds(pl.multiple_of(g * group_rows, group_rows), group_rows)
        return remote(
            stage.at[:, here, pl.ds(lane(j - kept), LANES)],
            mult_ref.at[:, here, pl.ds(lane(j), LANES)],
            result_send.at[g, j], result_recv.at[g, j], end, core,
        )

    def multiply(first, count, j, out, out_row, out_lane):
        here = pl.ds(first, count)
        column = pl.ds(lane(j), LANES)
        right = jnp.concatenate([grid[0, :, column], grid[1, :, column]], axis=1)
        by_re = jnp.dot(grid[0, here, :], right, preferred_element_type=jnp.float32)
        by_im = jnp.dot(grid[1, here, :], right, preferred_element_type=jnp.float32)
        mult_re = (by_re[:, :LANES] - by_im[:, LANES:]) * factor
        mult_im = (by_re[:, LANES:] + by_im[:, :LANES]) * factor
        out[0, pl.ds(out_row, count), pl.ds(out_lane, LANES)] = mult_re
        out[1, pl.ds(out_row, count), pl.ds(out_lane, LANES)] = mult_im
        data_re = grid[0, here, column].astype(jnp.float32)
        data_im = grid[1, here, column].astype(jnp.float32)
        for i, term in enumerate((
            mult_re * data_re + mult_im * data_im,
            mult_re * data_im - mult_im * data_re,
            mult_re * mult_re + mult_im * mult_im,
        )):
            acc[pl.ds(i * 8, 8), :] += jnp.sum(term.reshape(count // 8, 8, LANES), axis=0)

    def own(j):
        multiply(row(z, core), rows, j, mult_ref, 0, lane(j))

    def loop(lower, upper, body):
        def run(j, carry):
            body(j)
            return carry
        lax.fori_loop(lower, upper, run, 0)

    def pack():
        sums = [jnp.sum(acc[pl.ds(8 * i, 8), :], axis=0, keepdims=True) for i in range(3)]
        return jnp.concatenate(sums + [jnp.zeros((5, LANES), jnp.float32)], axis=0)

    def give(slot, device):
        return pltpu.make_async_remote_copy(
            src_ref=packed.at[slot], dst_ref=partial_in.at[slot],
            send_sem=sum_send.at[slot], recv_sem=sum_recv.at[slot],
            device_id=device, device_id_type=MESH,
        )

    def give_total():
        return remote(total_ref, total_ref, sum_send.at[5], sum_recv.at[5], end, core)

    mine = grid.at[:, pl.ds(row(z, core), rows), :]
    load = pltpu.make_async_copy(traces_ref.at[:, 0], mine, load_sem)
    load.start()
    acc[...] = jnp.zeros_like(acc)

    barrier = pltpu.get_barrier_semaphore()

    def greet(f, s):
        pl.semaphore_signal(barrier, inc=1, device_id=(f, s), device_id_type=MESH)

    greet(freq, z * 2 + 1 - core)

    @pl.when(is_end)
    def _():
        greet(freq, mid * 2 + core)
        pl.semaphore_wait(barrier, 2)

    @pl.when(jnp.logical_not(is_end))
    def _():
        greet(freq, end * 2 + core)
        greet(freq, far_mid * 2 + core)
        greet(beside, shot)
        greet(across, shot)
        pl.semaphore_wait(barrier, 5)

    load.wait()

    @pl.when(is_end)
    def _():
        for d in range(len(schedule)):
            piece(d).start()
        loop(0, kept, lambda j: pair(z, j, 3).start())

        def work(j):
            for slot, chip in enumerate((mid, far_mid, far_end)):
                arrived(chip, j, slot)
                pair(chip, j, slot).start()
            for slot, chip in enumerate((mid, far_mid, far_end, end)):
                paired(chip, j, slot)
            own(j)

        loop(0, kept, work)
        packed[0] = pack()
        give(0, (freq, mid * 2 + core)).start()

        def settle(j):
            for slot, chip in enumerate((mid, far_mid, far_end, end)):
                pair(chip, j, slot).wait_send()

        loop(0, kept, settle)
        for d in range(len(schedule)):
            piece(d).wait_send()
        give(0, (freq, mid * 2 + core)).wait_send()

        def take(j):
            loop(0, groups, lambda g: result(g, j).wait_recv())

        loop(kept, chunks, take)
        give_total().wait_recv()

    @pl.when(jnp.logical_not(is_end))
    def _():
        def own_sends(j):
            to_far(z, j, 0).start()

            @pl.when(j < kept)
            def _():
                to_end(z, j, 0).start()
            pair(z, j, 3).start()

        def near(j):
            to_far(end, j, 1).start()
            pair(end, j, 0).start()

        def take_pieces(i):
            for d in range(len(schedule)):
                @pl.when(i == schedule[d][4])
                def _(d=d):
                    piece(d).wait_recv()

        own_sends(0)
        own_sends(1)
        for d in range(len(schedule)):
            if schedule[d][4] < 0:
                piece(d).wait_recv()
        near(0)
        near(1)

        def work(j):
            for slot, chip in ((1, far_mid), (2, far_end)):
                arrived(chip, j, slot)

                @pl.when(j < kept)
                def _():
                    to_end(chip, j, slot).start()
                pair(chip, j, slot).start()
            take_pieces(j)

            @pl.when(j + 2 < chunks)
            def _():
                own_sends(j + 2)
                near(j + 2)
            for slot, chip in ((0, end), (1, far_mid), (2, far_end), (3, z)):
                paired(chip, j, slot)

            def group(g):
                at = ready[0]
                for k in range(1, groups):
                    at = jnp.where(g >= k, ready[k], at)
                lower = jnp.where(j == at, kept, j)
                upper = jnp.where(j >= at, j + 1, lower)

                def task(jj):
                    multiply(
                        pl.multiple_of(row(end, core) + g * group_rows, group_rows), group_rows, jj,
                        stage, pl.multiple_of(g * group_rows, group_rows), lane(jj - kept),
                    )
                    result(g, jj).start()

                loop(lower, upper, task)

            loop(0, groups, group)
            own(j)

        loop(0, chunks, work)

        give(0, (freq, end * 2 + core)).wait_recv()
        total = pack() + partial_in[0]
        for slot, device in enumerate((
            (freq, z * 2 + 1 - core), (freq, far_mid * 2 + core), (beside, shot), (across, shot),
        )):
            packed[slot + 1] = total
            give(slot + 1, device).start()
            give(slot + 1, device).wait_recv()
            total = total + partial_in[slot + 1]
        total_ref[...] = total
        give_total().start()

        def drain(j):
            to_far(z, j, 0).wait_send()
            to_far(end, j, 1).wait_send()
            for slot, chip in enumerate((end, far_mid, far_end, z)):
                pair(chip, j, slot).wait_send()

            @pl.when(j < kept)
            def _():
                for slot, chip in enumerate((z, far_mid, far_end)):
                    to_end(chip, j, slot).wait_send()

            @pl.when(j >= kept)
            def _():
                loop(0, groups, lambda g: result(g, j).wait_send())

        loop(0, chunks, drain)
        for slot, device in enumerate((
            (freq, z * 2 + 1 - core), (freq, far_mid * 2 + core), (beside, shot), (across, shot),
        )):
            give(slot + 1, device).wait_send()
        give_total().wait_send()


def epilogue_kernel(
    total_count, strip, width, total_ref, traces_ref, mult_ref, multiples_ref, primaries_ref,
    multiples, primaries, fit, sems,
):
    rows, order = mult_ref.shape[1], mult_ref.shape[2]
    num_re, num_im, denom = (jnp.sum(total_ref[pl.ds(i, 1), :]) for i in range(3))
    scaled_den = denom / total_count + epsilon
    fit_re = num_re / total_count / scaled_den
    fit_im = num_im / total_count / scaled_den

    def copies(s):
        here = pl.ds(pl.multiple_of(s * strip, strip), strip)
        return (
            pltpu.make_async_copy(multiples.at[:, here, :], multiples_ref.at[:, 0, here, :], sems.at[0, s]),
            pltpu.make_async_copy(primaries.at[:, here, :], primaries_ref.at[:, 0, here, :], sems.at[1, s]),
        )

    def part(s, carry):
        here = pl.ds(pl.multiple_of(s * strip, strip), strip)
        for q in range(order // width):
            columns = pl.ds(q * width, width)
            mult_re = mult_ref[0, here, columns]
            mult_im = mult_ref[1, here, columns]
            data_re = traces_ref[0, 0, here, columns].astype(jnp.float32)
            data_im = traces_ref[1, 0, here, columns].astype(jnp.float32)
            prim_re = data_re - (fit_re * mult_re - fit_im * mult_im)
            prim_im = data_im - (fit_re * mult_im + fit_im * mult_re)
            multiples[0, here, columns] = mult_re.astype(jnp.bfloat16)
            multiples[1, here, columns] = mult_im.astype(jnp.bfloat16)
            primaries[0, here, columns] = prim_re.astype(jnp.bfloat16)
            primaries[1, here, columns] = prim_im.astype(jnp.bfloat16)
        for copy in copies(s):
            copy.start()
        return carry

    lax.fori_loop(0, rows // strip, part, 0)

    def wait(s, carry):
        for copy in copies(s):
            copy.wait()
        return carry

    lax.fori_loop(0, rows // strip, wait, 0)


def on_a_line(traces):
    rows, order = traces.shape[2], traces.shape[3]
    freqs = lax.axis_size("freq")
    chunks = order // LANES
    groups = 3
    kept = max(1, round(0.22 * chunks))
    ready = tuple(max(kept, round(f * chunks)) for f in (0.29, 0.42, 0.5))
    schedule = end_schedule(chunks, groups, ready)
    pieces = len(schedule)
    dma = pltpu.SemaphoreType.DMA
    mult, totals = pl.pallas_call(
        functools.partial(line_kernel, chunks, kept, groups, ready, schedule, freqs),
        out_shape=(
            pltpu.VMEM((2, rows, order), jnp.float32),
            pltpu.VMEM((8, LANES), jnp.float32),
        ),
        in_specs=[pl.BlockSpec(memory_space=pltpu.HBM)],
        out_specs=(
            pl.BlockSpec(memory_space=pltpu.VMEM),
            pl.BlockSpec(memory_space=pltpu.VMEM),
        ),
        scratch_shapes=[
            pltpu.VMEM((2, order, order), jnp.bfloat16),
            pltpu.VMEM((2, rows, (chunks - kept) * LANES), jnp.float32),
            pltpu.VMEM((24, LANES), jnp.float32),
            pltpu.VMEM((5, 8, LANES), jnp.float32),
            pltpu.VMEM((5, 8, LANES), jnp.float32),
            dma, dma((pieces,)), dma((pieces,)), dma((3, chunks)), dma((2, chunks)),
            dma((3, kept)), dma((4, chunks)), dma((4, chunks)),
            dma((groups, chunks)), dma((groups, chunks)), dma((6,)), dma((6,)),
        ],
        compiler_params=pltpu.CompilerParams(
            collective_id=0, has_side_effects=True, vmem_limit_bytes=48 * 1024 * 1024
        ),
    )(traces)
    strip = 16
    out = jax.ShapeDtypeStruct(traces.shape, traces.dtype)
    whole = pl.BlockSpec(memory_space=pltpu.VMEM)
    away = pl.BlockSpec(memory_space=pltpu.HBM)
    return pl.pallas_call(
        functools.partial(epilogue_kernel, float(freqs * order * order), strip, 4 * LANES),
        out_shape=(out, out),
        in_specs=[whole, whole, whole],
        out_specs=(away, away),
        scratch_shapes=[
            pltpu.VMEM((2, rows, order), jnp.bfloat16),
            pltpu.VMEM((2, rows, order), jnp.bfloat16),
            pltpu.SMEM((2,), jnp.float32),
            dma((2, rows // strip)),
        ],
        compiler_params=pltpu.CompilerParams(vmem_limit_bytes=24 * 1024 * 1024),
    )(totals, traces, mult)


def solution(mesh):
    placed = P(None, "freq", "shot", None)

    def per_device(traces):
        four_chips = mesh.shape["shot"] == 2 * 4 and mesh.shape["freq"] == 4
        rows, order = traces.shape[2], traces.shape[3]
        fits = rows % 48 == 0 and order % (4 * LANES) == 0
        if four_chips and traces.shape[1] == 1 and fits:
            return on_a_line(traces)
        return gathered(traces)

    return jax.shard_map(
        per_device, mesh=mesh, in_specs=(placed,), out_specs=(placed, placed), check_vma=False
    )
```

time: 271 us -> 262 us (0.967)
  Pallas kernels: 269 us -> 261 us
    pallas_call x1, Pallas kernels: 262 us -> 257 us  [on_a_line(): pl.pallas_call(functools.partial(line_kernel, chunks, kept, groups, ready...]
    pallas_call x1, Pallas kernels: 7.18 us -> 4.21 us  [on_a_line(): pl.pallas_call(functools.partial(epilogue_kernel, float(freqs * order * o...]
where the time goes in v1:
time: 262 us
  Pallas kernels  261 us (100%)
    pallas_call x1, Pallas kernels, on_a_line(): pl.pallas_call(functools.partial(line_kernel, chunks, kept, groups, ready...  257 us

profile of v1, /device:TPU:1, one launch (start us, length us, event | category | flops | bytes accessed | tf_op | source)
XLA Modules:
  0.0 261.8 jit_solution(1063213363636481421)
XLA Ops:
  0.6 0.0 copy-start
  0.6 257.0 %shard_map.30 = (f32[2,384,3072]{2,1,0:T(8,128)S(1)}, f32[8,128]{1,0:T(8,128)S(1)}) custom-call(bf16[2,1,384,3072]{3,2,1,0:T(8,128)(2,1)} %traces_ref.3), custom_call_target="tpu_custom_call" | custom-call | tf_op jit(solution)/shard_map/pallas_call | solution.py:432
  257.6 0.0 copy-done
  257.6 4.2 %shard_map.31 = (bf16[2,1,384,3072]{3,2,1,0:T(8,128)(2,1)}, bf16[2,1,384,3072]{3,2,1,0:T(8,128)(2,1)}) custom-call(f32[8,128]{1,0:T(8,128)S(1)} %get-tuple-element.4.total_ref, bf16[2,1,384,3072]{3,2,1,0:T(8,128)(2,1)S(1)} %copy-done, f32[2,384,3072]{2,1,0:T(8,128)S(1)} %get-tuple-element.5.mult_ref), custom_call_target="tpu_custom_call" | custom-call | tf_op jit(solution)/shard_map/pallas_call | solution.py:461
Async XLA Ops:
  0.6 257.0 %copy-start = (bf16[2,1,384,3072]{3,2,1,0:T(8,128)(2,1)S(1)}, bf16[2,1,384,3072]{3,2,1,0:T(8,128)(2,1)}, u32[]{:S(2)}) copy-start(bf16[2,1,384,3072]{3,2,1,0:T(8,128)(2,1)} %traces_ref.3) | copy-start | bytes 14155780

commit v2 on v1

--- a/solution.py
+++ b/solution.py
@@ -57,26 +57,27 @@
 
 
 def end_schedule(chunks, groups, ready):
+    half, most = chunks // 2, 3 * chunks // 4
     done = [0] * chunks
     pieces = []
 
     def column(c):
-        if done[c] < groups:
-            pieces.append((done[c], groups - done[c], c, 1))
-            left = groups - done[c]
+        left = groups - done[c]
+        if left:
+            pieces.append((done[c], left, c, 1))
             done[c] = groups
-            return left
-        return 0
+        return left
 
     window = 2 * groups
     room = window - column(0) - column(1)
     following = 2
-    while min(done) < groups:
-        while room > 0 and min(done) < groups:
-            group = min(done)
+    while min(done[:most]) < groups:
+        while room > 0 and min(done[:most]) < groups:
+            group = min(done[:most])
             first = done.index(group)
+            bound = half if first < half else most
             last = first
-            while last < chunks and done[last] == group and last - first < room:
+            while last < bound and done[last] == group and last - first < room:
                 last += 1
             pieces.append((group, 1, first, last - first))
             done[first:last] = [group + 1] * (last - first)
@@ -85,11 +86,13 @@
         if following < chunks:
             room -= column(following)
             following += 1
+    step = max(1, (chunks - most) // 2)
+    pieces += [(0, groups, c, min(step, chunks - c)) for c in range(most, chunks, step)]
     out = []
     for group, count, first, width in pieces:
-        column_need = first - 2
-        group_need = min(ready[g] for g in range(group, group + count))
-        out.append((group, count, first, width, max(-1, min(column_need, group_need))))
+        column_need = 2 * (first - 2) + 1
+        group_need = min(2 * ready[g] for g in range(group, group + count)) if first < most else chunks - 1
+        out.append((group, count, first, width, max(-1, min(column_need, group_need, chunks - 1))))
     return tuple(out)
 
 
@@ -98,11 +101,12 @@
     traces_ref, mult_ref, total_ref,
     grid, stage, acc, packed, partial_in,
     load_sem, piece_send, piece_recv, ici_recv, far_send, end_send, pair_send, pair_recv,
-    result_send, result_recv, sum_send, sum_recv,
+    result_send, result_recv, full_send, full_recv, sum_send, sum_recv,
 ):
     rows = traces_ref.shape[2]
     order = traces_ref.shape[3]
     group_rows = rows // groups
+    half, quarter = chunks // 2, chunks // 4
     factor = 1.0 / math.sqrt(order)
     freq = lax.axis_index("freq")
     shot = lax.axis_index("shot")
@@ -117,6 +121,18 @@
     beside = freq + 1 - 2 * (freq % 2)
     across = (freq + 2) % freqs
 
+    def first_last(i):
+        return (i + quarter) % chunks
+
+    def first_third(i):
+        return jnp.where(i < half, i + quarter, jnp.where(i < 3 * quarter, i - half, i))
+
+    def sent(i):
+        return jnp.where(low, first_last(i), first_third(i))
+
+    def taken(i):
+        return jnp.where(low, first_third(i), first_last(i))
+
     def row(chip, plane):
         return pl.multiple_of((chip * 2 + plane) * rows, rows)
 
@@ -159,28 +175,42 @@
         ref = grid.at[
             :,
             pl.ds(pl.multiple_of(row(end, core) + group * group_rows, group_rows), count * group_rows),
-            pl.ds(first * LANES, width * LANES),
+            pl.ds(lane(sent(first)), width * LANES),
         ]
         return remote(ref, ref, piece_send.at[d], piece_recv.at[d], mid, core)
 
-    def result(g, j):
+    def result(g, i):
         here = pl.ds(pl.multiple_of(g * group_rows, group_rows), group_rows)
         return remote(
-            stage.at[:, here, pl.ds(lane(j - kept), LANES)],
-            mult_ref.at[:, here, pl.ds(lane(j), LANES)],
-            result_send.at[g, j], result_recv.at[g, j], end, core,
+            stage.at[:, here, pl.ds(lane(i - kept), LANES)],
+            mult_ref.at[:, here, pl.ds(lane(taken(i)), LANES)],
+            result_send.at[g, i], result_recv.at[g, i], end, core,
         )
 
-    def multiply(first, count, j, out, out_row, out_lane):
+    def full(i):
+        return remote(
+            stage.at[:, :, pl.ds(lane(i - kept), LANES)],
+            mult_ref.at[:, :, pl.ds(lane(taken(i)), LANES)],
+            full_send.at[i - half], full_recv.at[i - half], end, core,
+        )
+
+    def multiply(first, count, j, inner, depth, out, out_row, out_lane, onto, fit):
         here = pl.ds(first, count)
         column = pl.ds(lane(j), LANES)
-        right = jnp.concatenate([grid[0, :, column], grid[1, :, column]], axis=1)
-        by_re = jnp.dot(grid[0, here, :], right, preferred_element_type=jnp.float32)
-        by_im = jnp.dot(grid[1, here, :], right, preferred_element_type=jnp.float32)
+        span = pl.ds(inner, depth)
+        right = jnp.concatenate([grid[0, span, column], grid[1, span, column]], axis=1)
+        by_re = jnp.dot(grid[0, here, span], right, preferred_element_type=jnp.float32)
+        by_im = jnp.dot(grid[1, here, span], right, preferred_element_type=jnp.float32)
         mult_re = (by_re[:, :LANES] - by_im[:, LANES:]) * factor
         mult_im = (by_re[:, LANES:] + by_im[:, :LANES]) * factor
-        out[0, pl.ds(out_row, count), pl.ds(out_lane, LANES)] = mult_re
-        out[1, pl.ds(out_row, count), pl.ds(out_lane, LANES)] = mult_im
+        to = pl.ds(out_row, count), pl.ds(out_lane, LANES)
+        if onto:
+            mult_re = mult_re + out[0, to[0], to[1]]
+            mult_im = mult_im + out[1, to[0], to[1]]
+        out[0, to[0], to[1]] = mult_re
+        out[1, to[0], to[1]] = mult_im
+        if not fit:
+            return
         data_re = grid[0, here, column].astype(jnp.float32)
         data_im = grid[1, here, column].astype(jnp.float32)
         for i, term in enumerate((
@@ -191,7 +221,7 @@
             acc[pl.ds(i * 8, 8), :] += jnp.sum(term.reshape(count // 8, 8, LANES), axis=0)
 
     def own(j):
-        multiply(row(z, core), rows, j, mult_ref, 0, lane(j))
+        multiply(row(z, core), rows, j, 0, order, mult_ref, 0, lane(j), False, True)
 
     def loop(lower, upper, body):
         def run(j, carry):
@@ -244,9 +274,10 @@
     def _():
         for d in range(len(schedule)):
             piece(d).start()
-        loop(0, kept, lambda j: pair(z, j, 3).start())
-
-        def work(j):
+        loop(0, half, lambda i: pair(z, taken(i), 3).start())
+
+        def work(i):
+            j = taken(i)
             for slot, chip in enumerate((mid, far_mid, far_end)):
                 arrived(chip, j, slot)
                 pair(chip, j, slot).start()
@@ -255,41 +286,53 @@
             own(j)
 
         loop(0, kept, work)
+
+        def complete(i):
+            j = taken(i)
+            paired(end, j, 3)
+            loop(0, groups, lambda g: result(g, i).wait_recv())
+            inner = pl.multiple_of(end * 2 * rows, 2 * rows)
+            multiply(row(z, core), rows, j, inner, 2 * rows, mult_ref, 0, lane(j), True, True)
+
+        loop(kept, half, complete)
         packed[0] = pack()
         give(0, (freq, mid * 2 + core)).start()
 
-        def settle(j):
-            for slot, chip in enumerate((mid, far_mid, far_end, end)):
-                pair(chip, j, slot).wait_send()
-
-        loop(0, kept, settle)
+        def settle(i):
+            pair(z, taken(i), 3).wait_send()
+
+            @pl.when(i < kept)
+            def _():
+                for slot, chip in enumerate((mid, far_mid, far_end)):
+                    pair(chip, taken(i), slot).wait_send()
+
+        loop(0, half, settle)
         for d in range(len(schedule)):
             piece(d).wait_send()
         give(0, (freq, mid * 2 + core)).wait_send()
-
-        def take(j):
-            loop(0, groups, lambda g: result(g, j).wait_recv())
-
-        loop(kept, chunks, take)
+        loop(half, chunks, lambda i: full(i).wait_recv())
         give_total().wait_recv()
 
     @pl.when(jnp.logical_not(is_end))
     def _():
-        def own_sends(j):
-            to_far(z, j, 0).start()
-
-            @pl.when(j < kept)
-            def _():
-                to_end(z, j, 0).start()
-            pair(z, j, 3).start()
-
-        def near(j):
-            to_far(end, j, 1).start()
-            pair(end, j, 0).start()
-
-        def take_pieces(i):
+        def own_sends(i):
+            to_far(z, sent(i), 0).start()
+
+            @pl.when(i < kept)
+            def _():
+                to_end(z, taken(i), 0).start()
+            pair(z, taken(i), 3).start()
+
+        def near(i):
+            to_far(end, sent(i), 1).start()
+
+            @pl.when(i < half)
+            def _():
+                pair(end, sent(i), 0).start()
+
+        def take_pieces(stop):
             for d in range(len(schedule)):
-                @pl.when(i == schedule[d][4])
+                @pl.when(stop == schedule[d][4])
                 def _(d=d):
                     piece(d).wait_recv()
 
@@ -301,40 +344,63 @@
         near(0)
         near(1)
 
-        def work(j):
-            for slot, chip in ((1, far_mid), (2, far_end)):
-                arrived(chip, j, slot)
-
-                @pl.when(j < kept)
-                def _():
-                    to_end(chip, j, slot).start()
-                pair(chip, j, slot).start()
-            take_pieces(j)
-
-            @pl.when(j + 2 < chunks)
-            def _():
-                own_sends(j + 2)
-                near(j + 2)
-            for slot, chip in ((0, end), (1, far_mid), (2, far_end), (3, z)):
-                paired(chip, j, slot)
-
+        inner = pl.multiple_of((1 - end // 3) * 2 * rows, 2 * rows)
+
+        def part(g, i):
+            first = pl.multiple_of(g * group_rows, group_rows)
+            multiply(
+                pl.multiple_of(row(end, core) + first, group_rows), group_rows, taken(i),
+                inner, order - 2 * rows, stage, first, lane(i - kept), False, False,
+            )
+            result(g, i).start()
+
+        def starts(g):
+            at = ready[0]
+            for k in range(1, groups):
+                at = jnp.where(g >= k, ready[k], at)
+            return at
+
+        def parts(i, step):
             def group(g):
-                at = ready[0]
-                for k in range(1, groups):
-                    at = jnp.where(g >= k, ready[k], at)
-                lower = jnp.where(j == at, kept, j)
-                upper = jnp.where(j >= at, j + 1, lower)
-
-                def task(jj):
-                    multiply(
-                        pl.multiple_of(row(end, core) + g * group_rows, group_rows), group_rows, jj,
-                        stage, pl.multiple_of(g * group_rows, group_rows), lane(jj - kept),
-                    )
-                    result(g, jj).start()
-
-                loop(lower, upper, task)
+                at = starts(g)
+                if step == 0:
+                    lower, upper = kept, jnp.where(i == at, i, kept)
+                else:
+                    lower, upper = i, jnp.where(jnp.logical_and(i >= at, i < half), i + 1, i)
+                loop(lower, upper, lambda ii: part(g, ii))
 
             loop(0, groups, group)
+
+        def work(i):
+            take_pieces(2 * i)
+            for step in range(2):
+                if step == 1:
+                    j = taken(i)
+                    for slot, chip in ((1, far_mid), (2, far_end)):
+                        arrived(chip, j, slot)
+
+                        @pl.when(i < kept)
+                        def _(slot=slot, chip=chip):
+                            to_end(chip, j, slot).start()
+                        pair(chip, j, slot).start()
+                    take_pieces(2 * i + 1)
+
+                    @pl.when(i + 2 < chunks)
+                    def _():
+                        own_sends(i + 2)
+                        near(i + 2)
+
+                    @pl.when(i == half - 1)
+                    def _():
+                        loop(half, chunks, lambda ii: pair(end, sent(ii), 0).start())
+                    for slot, chip in ((0, end), (1, far_mid), (2, far_end), (3, z)):
+                        paired(chip, j, slot)
+                parts(i, step)
+
+            @pl.when(i >= half)
+            def _():
+                multiply(row(end, core), rows, j, 0, order, stage, 0, lane(i - kept), False, True)
+                full(i).start()
             own(j)
 
         loop(0, chunks, work)
@@ -351,20 +417,24 @@
         total_ref[...] = total
         give_total().start()
 
-        def drain(j):
-            to_far(z, j, 0).wait_send()
-            to_far(end, j, 1).wait_send()
+        def drain(i):
+            to_far(z, sent(i), 0).wait_send()
+            to_far(end, sent(i), 1).wait_send()
             for slot, chip in enumerate((end, far_mid, far_end, z)):
-                pair(chip, j, slot).wait_send()
-
-            @pl.when(j < kept)
+                pair(chip, taken(i), slot).wait_send()
+
+            @pl.when(i < kept)
             def _():
                 for slot, chip in enumerate((z, far_mid, far_end)):
-                    to_end(chip, j, slot).wait_send()
-
-            @pl.when(j >= kept)
-            def _():
-                loop(0, groups, lambda g: result(g, j).wait_send())
+                    to_end(chip, taken(i), slot).wait_send()
+
+            @pl.when(jnp.logical_and(i >= kept, i < half))
+            def _():
+                loop(0, groups, lambda g: result(g, i).wait_send())
+
+            @pl.when(i >= half)
+            def _():
+                full(i).wait_send()
 
         loop(0, chunks, drain)
         for slot, device in enumerate((
@@ -424,8 +494,9 @@
     freqs = lax.axis_size("freq")
     chunks = order // LANES
     groups = 3
-    kept = max(1, round(0.22 * chunks))
-    ready = tuple(max(kept, round(f * chunks)) for f in (0.29, 0.42, 0.5))
+    half = chunks // 2
+    kept = max(1, round(0.21 * chunks))
+    ready = tuple(min(half - 1, max(kept, round(f * chunks))) for f in (0.2, 0.29, 0.34))
     schedule = end_schedule(chunks, groups, ready)
     pieces = len(schedule)
     dma = pltpu.SemaphoreType.DMA
@@ -447,8 +518,8 @@
             pltpu.VMEM((5, 8, LANES), jnp.float32),
             pltpu.VMEM((5, 8, LANES), jnp.float32),
             dma, dma((pieces,)), dma((pieces,)), dma((3, chunks)), dma((2, chunks)),
-            dma((3, kept)), dma((4, chunks)), dma((4, chunks)),
-            dma((groups, chunks)), dma((groups, chunks)), dma((6,)), dma((6,)),
+            dma((3, chunks)), dma((4, chunks)), dma((4, chunks)),
+            dma((groups, half)), dma((groups, half)), dma((half,)), dma((half,)), dma((6,)), dma((6,)),
         ],
         compiler_params=pltpu.CompilerParams(
             collective_id=0, has_side_effects=True, vmem_limit_bytes=48 * 1024 * 1024

time: 262 us -> 242 us (0.924)
  Pallas kernels: 261 us -> 240 us
    pallas_call x1, Pallas kernels: 257 us -> 235 us  [on_a_line(): pl.pallas_call(functools.partial(line_kernel, chunks, kept, groups, ready...]
where the time goes in v2:
time: 242 us; the launch traced here: 240 us
  Pallas kernels  240 us (99%)
    pallas_call x1, Pallas kernels, on_a_line(): pl.pallas_call(functools.partial(line_kernel, chunks, kept, groups, ready...  235 us

profile of v2, /device:TPU:1, one launch (start us, length us, event | category | flops | bytes accessed | tf_op | source)
XLA Modules:
  0.0 240.3 jit_solution(18217836250365149158)
XLA Ops:
  0.6 0.0 copy-start
  0.6 235.5 %shard_map.30 = (f32[2,384,3072]{2,1,0:T(8,128)S(1)}, f32[8,128]{1,0:T(8,128)S(1)}) custom-call(bf16[2,1,384,3072]{3,2,1,0:T(8,128)(2,1)} %traces_ref.3), custom_call_target="tpu_custom_call" | custom-call | tf_op jit(solution)/shard_map/pallas_call | solution.py:503
  236.1 0.0 copy-done
  236.1 4.2 %shard_map.31 = (bf16[2,1,384,3072]{3,2,1,0:T(8,128)(2,1)}, bf16[2,1,384,3072]{3,2,1,0:T(8,128)(2,1)}) custom-call(f32[8,128]{1,0:T(8,128)S(1)} %get-tuple-element.4.total_ref, bf16[2,1,384,3072]{3,2,1,0:T(8,128)(2,1)S(1)} %copy-done, f32[2,384,3072]{2,1,0:T(8,128)S(1)} %get-tuple-element.5.mult_ref), custom_call_target="tpu_custom_call" | custom-call | tf_op jit(solution)/shard_map/pallas_call | solution.py:532
Async XLA Ops:
  0.6 235.5 %copy-start = (bf16[2,1,384,3072]{3,2,1,0:T(8,128)(2,1)S(1)}, bf16[2,1,384,3072]{3,2,1,0:T(8,128)(2,1)}, u32[]{:S(2)}) copy-start(bf16[2,1,384,3072]{3,2,1,0:T(8,128)(2,1)} %traces_ref.3) | copy-start | bytes 14155780

commit v3 on v2

--- a/solution.py
+++ b/solution.py
@@ -56,32 +56,35 @@
     return finish(traces, mult_re, mult_im, sums[0], sums[1], sums[2])
 
 
-def end_schedule(chunks, groups, ready):
+def end_schedule(chunks, sizes, ready):
+    groups = len(sizes)
     half, most = chunks // 2, 3 * chunks // 4
     done = [0] * chunks
     pieces = []
 
     def column(c):
-        left = groups - done[c]
+        left = sum(sizes[done[c]:])
         if left:
-            pieces.append((done[c], left, c, 1))
+            pieces.append((done[c], groups - done[c], c, 1))
             done[c] = groups
         return left
 
-    window = 2 * groups
+    window = 2 * sum(sizes)
     room = window - column(0) - column(1)
     following = 2
     while min(done[:most]) < groups:
-        while room > 0 and min(done[:most]) < groups:
+        while min(done[:most]) < groups:
             group = min(done[:most])
             first = done.index(group)
             bound = half if first < half else most
             last = first
-            while last < bound and done[last] == group and last - first < room:
+            while last < bound and done[last] == group and (last - first + 1) * sizes[group] <= room:
                 last += 1
+            if last == first:
+                break
             pieces.append((group, 1, first, last - first))
             done[first:last] = [group + 1] * (last - first)
-            room -= last - first
+            room -= (last - first) * sizes[group]
         room += window
         if following < chunks:
             room -= column(following)
@@ -97,7 +100,7 @@
 
 
 def line_kernel(
-    chunks, kept, groups, ready, schedule, freqs,
+    chunks, kept, sizes, ready, schedule, freqs,
     traces_ref, mult_ref, total_ref,
     grid, stage, acc, packed, partial_in,
     load_sem, piece_send, piece_recv, ici_recv, far_send, end_send, pair_send, pair_recv,
@@ -105,7 +108,8 @@
 ):
     rows = traces_ref.shape[2]
     order = traces_ref.shape[3]
-    group_rows = rows // groups
+    groups = len(sizes)
+    firsts = [sum(sizes[:g]) for g in range(groups)]
     half, quarter = chunks // 2, chunks // 4
     factor = 1.0 / math.sqrt(order)
     freq = lax.axis_index("freq")
@@ -174,13 +178,13 @@
         group, count, first, width, _ = schedule[d]
         ref = grid.at[
             :,
-            pl.ds(pl.multiple_of(row(end, core) + group * group_rows, group_rows), count * group_rows),
+            pl.ds(pl.multiple_of(row(end, core) + firsts[group], 16), sum(sizes[group:group + count])),
             pl.ds(lane(sent(first)), width * LANES),
         ]
         return remote(ref, ref, piece_send.at[d], piece_recv.at[d], mid, core)
 
     def result(g, i):
-        here = pl.ds(pl.multiple_of(g * group_rows, group_rows), group_rows)
+        here = pl.ds(firsts[g], sizes[g])
         return remote(
             stage.at[:, here, pl.ds(lane(i - kept), LANES)],
             mult_ref.at[:, here, pl.ds(lane(taken(i)), LANES)],
@@ -290,7 +294,8 @@
         def complete(i):
             j = taken(i)
             paired(end, j, 3)
-            loop(0, groups, lambda g: result(g, i).wait_recv())
+            for g in range(groups):
+                result(g, i).wait_recv()
             inner = pl.multiple_of(end * 2 * rows, 2 * rows)
             multiply(row(z, core), rows, j, inner, 2 * rows, mult_ref, 0, lane(j), True, True)
 
@@ -317,10 +322,6 @@
     def _():
         def own_sends(i):
             to_far(z, sent(i), 0).start()
-
-            @pl.when(i < kept)
-            def _():
-                to_end(z, taken(i), 0).start()
             pair(z, taken(i), 3).start()
 
         def near(i):
@@ -336,8 +337,10 @@
                 def _(d=d):
                     piece(d).wait_recv()
 
+        lead = min(3, kept)
         own_sends(0)
         own_sends(1)
+        loop(0, lead, lambda i: to_end(z, taken(i), 0).start())
         for d in range(len(schedule)):
             if schedule[d][4] < 0:
                 piece(d).wait_recv()
@@ -347,60 +350,53 @@
         inner = pl.multiple_of((1 - end // 3) * 2 * rows, 2 * rows)
 
         def part(g, i):
-            first = pl.multiple_of(g * group_rows, group_rows)
             multiply(
-                pl.multiple_of(row(end, core) + first, group_rows), group_rows, taken(i),
-                inner, order - 2 * rows, stage, first, lane(i - kept), False, False,
+                pl.multiple_of(row(end, core) + firsts[g], 16), sizes[g], taken(i),
+                inner, order - 2 * rows, stage, firsts[g], lane(i - kept), False, False,
             )
             result(g, i).start()
 
-        def starts(g):
-            at = ready[0]
-            for k in range(1, groups):
-                at = jnp.where(g >= k, ready[k], at)
-            return at
-
-        def parts(i, step):
-            def group(g):
-                at = starts(g)
-                if step == 0:
-                    lower, upper = kept, jnp.where(i == at, i, kept)
-                else:
-                    lower, upper = i, jnp.where(jnp.logical_and(i >= at, i < half), i + 1, i)
-                loop(lower, upper, lambda ii: part(g, ii))
-
-            loop(0, groups, group)
+        def parts(lowers, uppers):
+            for g in range(groups):
+                loop(lowers[g], uppers[g], functools.partial(part, g))
 
         def work(i):
             take_pieces(2 * i)
-            for step in range(2):
-                if step == 1:
-                    j = taken(i)
-                    for slot, chip in ((1, far_mid), (2, far_end)):
-                        arrived(chip, j, slot)
-
-                        @pl.when(i < kept)
-                        def _(slot=slot, chip=chip):
-                            to_end(chip, j, slot).start()
-                        pair(chip, j, slot).start()
-                    take_pieces(2 * i + 1)
-
-                    @pl.when(i + 2 < chunks)
-                    def _():
-                        own_sends(i + 2)
-                        near(i + 2)
-
-                    @pl.when(i == half - 1)
-                    def _():
-                        loop(half, chunks, lambda ii: pair(end, sent(ii), 0).start())
-                    for slot, chip in ((0, end), (1, far_mid), (2, far_end), (3, z)):
-                        paired(chip, j, slot)
-                parts(i, step)
+            parts([kept] * groups, [jnp.where(i == at, i, kept) for at in ready])
+
+            j = taken(i)
+            for slot, chip in ((1, far_mid), (2, far_end)):
+                arrived(chip, j, slot)
+
+                @pl.when(i < kept)
+                def _(slot=slot, chip=chip):
+                    to_end(chip, j, slot).start()
+                pair(chip, j, slot).start()
+
+            @pl.when(i + lead < kept)
+            def _():
+                to_end(z, taken(i + lead), 0).start()
+
+            @pl.when(i + 2 < chunks)
+            def _():
+                own_sends(i + 2)
+            for slot, chip in ((0, end), (1, far_mid), (2, far_end), (3, z)):
+                paired(chip, j, slot)
+            parts([i] * groups, [jnp.where(jnp.logical_and(i >= at, i < half), i + 1, i) for at in ready])
 
             @pl.when(i >= half)
             def _():
                 multiply(row(end, core), rows, j, 0, order, stage, 0, lane(i - kept), False, True)
                 full(i).start()
+            take_pieces(2 * i + 1)
+
+            @pl.when(i + 2 < chunks)
+            def _():
+                near(i + 2)
+
+            @pl.when(i == half - 1)
+            def _():
+                loop(half, chunks, lambda ii: pair(end, sent(ii), 0).start())
             own(j)
 
         loop(0, chunks, work)
@@ -430,7 +426,8 @@
 
             @pl.when(jnp.logical_and(i >= kept, i < half))
             def _():
-                loop(0, groups, lambda g: result(g, i).wait_send())
+                for g in range(groups):
+                    result(g, i).wait_send()
 
             @pl.when(i >= half)
             def _():
@@ -493,15 +490,16 @@
     rows, order = traces.shape[2], traces.shape[3]
     freqs = lax.axis_size("freq")
     chunks = order // LANES
-    groups = 3
     half = chunks // 2
-    kept = max(1, round(0.21 * chunks))
-    ready = tuple(min(half - 1, max(kept, round(f * chunks))) for f in (0.2, 0.29, 0.34))
-    schedule = end_schedule(chunks, groups, ready)
+    kept = max(1, round(5 * chunks / 24))
+    sizes = tuple(part * (rows // 24) for part in (8, 8, 8))
+    groups = len(sizes)
+    ready = tuple(min(half - 1, max(kept, round(f * chunks / 24))) for f in (5, 6, 8))
+    schedule = end_schedule(chunks, sizes, ready)
     pieces = len(schedule)
     dma = pltpu.SemaphoreType.DMA
     mult, totals = pl.pallas_call(
-        functools.partial(line_kernel, chunks, kept, groups, ready, schedule, freqs),
+        functools.partial(line_kernel, chunks, kept, sizes, ready, schedule, freqs),
         out_shape=(
             pltpu.VMEM((2, rows, order), jnp.float32),
             pltpu.VMEM((8, LANES), jnp.float32),
@@ -525,7 +523,7 @@
             collective_id=0, has_side_effects=True, vmem_limit_bytes=48 * 1024 * 1024
         ),
     )(traces)
-    strip = 16
+    strip = 32
     out = jax.ShapeDtypeStruct(traces.shape, traces.dtype)
     whole = pl.BlockSpec(memory_space=pltpu.VMEM)
     away = pl.BlockSpec(memory_space=pltpu.HBM)
@@ -550,7 +548,7 @@
     def per_device(traces):
         four_chips = mesh.shape["shot"] == 2 * 4 and mesh.shape["freq"] == 4
         rows, order = traces.shape[2], traces.shape[3]
-        fits = rows % 48 == 0 and order % (4 * LANES) == 0
+        fits = rows % 384 == 0 and order % (4 * LANES) == 0
         if four_chips and traces.shape[1] == 1 and fits:
             return on_a_line(traces)
         return gathered(traces)

time: 242 us -> 239 us (0.988)
  no operation moved by 1% of the time
where the time goes in v3:
time: 239 us
  Pallas kernels  238 us (100%)
    pallas_call x1, Pallas kernels, on_a_line(): pl.pallas_call(functools.partial(line_kernel, chunks, kept, sizes, ready,...  234 us

profile of v3, /device:TPU:1, one launch (start us, length us, event | category | flops | bytes accessed | tf_op | source)
XLA Modules:
  0.0 239.2 jit_solution(13006434299173743605)
XLA Ops:
  0.6 0.0 copy-start
  0.6 234.4 %shard_map.30 = (f32[2,384,3072]{2,1,0:T(8,128)S(1)}, f32[8,128]{1,0:T(8,128)S(1)}) custom-call(bf16[2,1,384,3072]{3,2,1,0:T(8,128)(2,1)} %traces_ref.3), custom_call_target="tpu_custom_call" | custom-call | tf_op jit(solution)/shard_map/pallas_call | solution.py:501
  235.1 0.0 copy-done
  235.1 4.1 %shard_map.31 = (bf16[2,1,384,3072]{3,2,1,0:T(8,128)(2,1)}, bf16[2,1,384,3072]{3,2,1,0:T(8,128)(2,1)}) custom-call(f32[8,128]{1,0:T(8,128)S(1)} %get-tuple-element.4.total_ref, bf16[2,1,384,3072]{3,2,1,0:T(8,128)(2,1)S(1)} %copy-done, f32[2,384,3072]{2,1,0:T(8,128)S(1)} %get-tuple-element.5.mult_ref), custom_call_target="tpu_custom_call" | custom-call | tf_op jit(solution)/shard_map/pallas_call | solution.py:530
Async XLA Ops:
  0.6 234.4 %copy-start = (bf16[2,1,384,3072]{3,2,1,0:T(8,128)(2,1)S(1)}, bf16[2,1,384,3072]{3,2,1,0:T(8,128)(2,1)}, u32[]{:S(2)}) copy-start(bf16[2,1,384,3072]{3,2,1,0:T(8,128)(2,1)} %traces_ref.3) | copy-start | bytes 14155780

commit v4 on v3

--- a/solution.py
+++ b/solution.py
@@ -101,7 +101,7 @@
 
 def line_kernel(
     chunks, kept, sizes, ready, schedule, freqs,
-    traces_ref, mult_ref, total_ref,
+    traces_ref, mult_ref, fit_ref,
     grid, stage, acc, packed, partial_in,
     load_sem, piece_send, piece_recv, ici_recv, far_send, end_send, pair_send, pair_recv,
     result_send, result_recv, full_send, full_recv, sum_send, sum_recv,
@@ -244,12 +244,22 @@
             device_id=device, device_id_type=MESH,
         )
 
-    def give_total():
-        return remote(total_ref, total_ref, sum_send.at[5], sum_recv.at[5], end, core)
-
-    mine = grid.at[:, pl.ds(row(z, core), rows), :]
-    load = pltpu.make_async_copy(traces_ref.at[:, 0], mine, load_sem)
-    load.start()
+    def give_fit():
+        return remote(fit_ref, fit_ref, sum_send.at[5], sum_recv.at[5], end, core)
+
+    early = min(3, half)
+
+    def load(part):
+        first, last = ((quarter, quarter + early), (quarter + early, chunks), (0, quarter))[part]
+        columns = pl.ds(first * LANES, (last - first) * LANES)
+        return pltpu.make_async_copy(
+            traces_ref.at[:, 0, :, columns],
+            grid.at[:, pl.ds(row(z, core), rows), columns],
+            load_sem.at[part],
+        )
+
+    for part in range(3):
+        load(part).start()
     acc[...] = jnp.zeros_like(acc)
 
     barrier = pltpu.get_barrier_semaphore()
@@ -272,12 +282,18 @@
         greet(across, shot)
         pl.semaphore_wait(barrier, 5)
 
-    load.wait()
+    load(0).wait()
+    at_once = [d for d in range(len(schedule)) if sum(schedule[d][2:4]) <= early]
 
     @pl.when(is_end)
     def _():
+        for d in at_once:
+            piece(d).start()
+        load(1).wait()
+        load(2).wait()
         for d in range(len(schedule)):
-            piece(d).start()
+            if d not in at_once:
+                piece(d).start()
         loop(0, half, lambda i: pair(z, taken(i), 3).start())
 
         def work(i):
@@ -316,7 +332,7 @@
             piece(d).wait_send()
         give(0, (freq, mid * 2 + core)).wait_send()
         loop(half, chunks, lambda i: full(i).wait_recv())
-        give_total().wait_recv()
+        give_fit().wait_recv()
 
     @pl.when(jnp.logical_not(is_end))
     def _():
@@ -337,10 +353,12 @@
                 def _(d=d):
                     piece(d).wait_recv()
 
-        lead = min(3, kept)
+        lead = min(early, kept)
         own_sends(0)
         own_sends(1)
         loop(0, lead, lambda i: to_end(z, taken(i), 0).start())
+        load(1).wait()
+        load(2).wait()
         for d in range(len(schedule)):
             if schedule[d][4] < 0:
                 piece(d).wait_recv()
@@ -410,8 +428,13 @@
             give(slot + 1, device).start()
             give(slot + 1, device).wait_recv()
             total = total + partial_in[slot + 1]
-        total_ref[...] = total
-        give_total().start()
+        num_re, num_im, denom = (jnp.sum(total[i:i + 1], axis=1, keepdims=True) for i in range(3))
+        total_count = float(freqs * order * order)
+        scaled_den = denom / total_count + epsilon
+        fit_re = jnp.broadcast_to(num_re / total_count / scaled_den, (1, LANES))
+        fit_im = jnp.broadcast_to(num_im / total_count / scaled_den, (1, LANES))
+        fit_ref[...] = jnp.concatenate([fit_re, fit_im, jnp.zeros((6, LANES), jnp.float32)], axis=0)
+        give_fit().start()
 
         def drain(i):
             to_far(z, sent(i), 0).wait_send()
@@ -438,52 +461,54 @@
             (freq, z * 2 + 1 - core), (freq, far_mid * 2 + core), (beside, shot), (across, shot),
         )):
             give(slot + 1, device).wait_send()
-        give_total().wait_send()
+        give_fit().wait_send()
 
 
 def epilogue_kernel(
-    total_count, strip, width, total_ref, traces_ref, mult_ref, multiples_ref, primaries_ref,
-    multiples, primaries, fit, sems,
+    strip, width, fit_ref, traces_ref, mult_ref, multiples_ref, primaries_ref,
+    multiples, primaries, sems,
 ):
     rows, order = mult_ref.shape[1], mult_ref.shape[2]
-    num_re, num_im, denom = (jnp.sum(total_ref[pl.ds(i, 1), :]) for i in range(3))
-    scaled_den = denom / total_count + epsilon
-    fit_re = num_re / total_count / scaled_den
-    fit_im = num_im / total_count / scaled_den
-
-    def copies(s):
-        here = pl.ds(pl.multiple_of(s * strip, strip), strip)
-        return (
-            pltpu.make_async_copy(multiples.at[:, here, :], multiples_ref.at[:, 0, here, :], sems.at[0, s]),
-            pltpu.make_async_copy(primaries.at[:, here, :], primaries_ref.at[:, 0, here, :], sems.at[1, s]),
-        )
-
-    def part(s, carry):
-        here = pl.ds(pl.multiple_of(s * strip, strip), strip)
+    spread = width // LANES
+
+    def here(s):
+        return pl.ds(pl.multiple_of(s * strip, strip), strip)
+
+    def copy(s, which):
+        src, dst = ((multiples, multiples_ref), (primaries, primaries_ref))[which]
+        return pltpu.make_async_copy(src.at[:, here(s), :], dst.at[:, 0, here(s), :], sems.at[which, s])
+
+    def round_off(s, carry):
         for q in range(order // width):
             columns = pl.ds(q * width, width)
-            mult_re = mult_ref[0, here, columns]
-            mult_im = mult_ref[1, here, columns]
-            data_re = traces_ref[0, 0, here, columns].astype(jnp.float32)
-            data_im = traces_ref[1, 0, here, columns].astype(jnp.float32)
+            for part in range(2):
+                multiples[part, here(s), columns] = mult_ref[part, here(s), columns].astype(jnp.bfloat16)
+        copy(s, 0).start()
+        return carry
+
+    def subtract(s, carry):
+        fit_re = jnp.concatenate([fit_ref[0:1, :]] * spread, axis=1)
+        fit_im = jnp.concatenate([fit_ref[1:2, :]] * spread, axis=1)
+        for q in range(order // width):
+            columns = pl.ds(q * width, width)
+            mult_re = mult_ref[0, here(s), columns]
+            mult_im = mult_ref[1, here(s), columns]
+            data_re = traces_ref[0, 0, here(s), columns].astype(jnp.float32)
+            data_im = traces_ref[1, 0, here(s), columns].astype(jnp.float32)
             prim_re = data_re - (fit_re * mult_re - fit_im * mult_im)
             prim_im = data_im - (fit_re * mult_im + fit_im * mult_re)
-            multiples[0, here, columns] = mult_re.astype(jnp.bfloat16)
-            multiples[1, here, columns] = mult_im.astype(jnp.bfloat16)
-            primaries[0, here, columns] = prim_re.astype(jnp.bfloat16)
-            primaries[1, here, columns] = prim_im.astype(jnp.bfloat16)
-        for copy in copies(s):
-            copy.start()
+            primaries[0, here(s), columns] = prim_re.astype(jnp.bfloat16)
+            primaries[1, here(s), columns] = prim_im.astype(jnp.bfloat16)
+        copy(s, 1).start()
         return carry
 
-    lax.fori_loop(0, rows // strip, part, 0)
-
     def wait(s, carry):
-        for copy in copies(s):
-            copy.wait()
+        copy(s, 0).wait()
+        copy(s, 1).wait()
         return carry
 
-    lax.fori_loop(0, rows // strip, wait, 0)
+    for step in (round_off, subtract, wait):
+        lax.fori_loop(0, rows // strip, step, 0)
 
 
 def on_a_line(traces):
@@ -498,7 +523,7 @@
     schedule = end_schedule(chunks, sizes, ready)
     pieces = len(schedule)
     dma = pltpu.SemaphoreType.DMA
-    mult, totals = pl.pallas_call(
+    mult, fit = pl.pallas_call(
         functools.partial(line_kernel, chunks, kept, sizes, ready, schedule, freqs),
         out_shape=(
             pltpu.VMEM((2, rows, order), jnp.float32),
@@ -515,7 +540,7 @@
             pltpu.VMEM((24, LANES), jnp.float32),
             pltpu.VMEM((5, 8, LANES), jnp.float32),
             pltpu.VMEM((5, 8, LANES), jnp.float32),
-            dma, dma((pieces,)), dma((pieces,)), dma((3, chunks)), dma((2, chunks)),
+            dma((3,)), dma((pieces,)), dma((pieces,)), dma((3, chunks)), dma((2, chunks)),
             dma((3, chunks)), dma((4, chunks)), dma((4, chunks)),
             dma((groups, half)), dma((groups, half)), dma((half,)), dma((half,)), dma((6,)), dma((6,)),
         ],
@@ -528,18 +553,17 @@
     whole = pl.BlockSpec(memory_space=pltpu.VMEM)
     away = pl.BlockSpec(memory_space=pltpu.HBM)
     return pl.pallas_call(
-        functools.partial(epilogue_kernel, float(freqs * order * order), strip, 4 * LANES),
+        functools.partial(epilogue_kernel, strip, 4 * LANES),
         out_shape=(out, out),
         in_specs=[whole, whole, whole],
         out_specs=(away, away),
         scratch_shapes=[
             pltpu.VMEM((2, rows, order), jnp.bfloat16),
             pltpu.VMEM((2, rows, order), jnp.bfloat16),
-            pltpu.SMEM((2,), jnp.float32),
             dma((2, rows // strip)),
         ],
         compiler_params=pltpu.CompilerParams(vmem_limit_bytes=24 * 1024 * 1024),
-    )(totals, traces, mult)
+    )(fit, traces, mult)
 
 
 def solution(mesh):

time: 239 us -> 238 us (level)
  no operation moved by 1% of the time
where the time goes in v4:
time: 238 us
  Pallas kernels  237 us (100%)
    pallas_call x1, Pallas kernels, on_a_line(): pl.pallas_call(functools.partial(line_kernel, chunks, kept, sizes, ready,...  233 us

profile of v4, /device:TPU:1, one launch (start us, length us, event | category | flops | bytes accessed | tf_op | source)
XLA Modules:
  0.0 237.7 jit_solution(15154605325233535171)
XLA Ops:
  0.6 0.0 copy-start
  0.6 233.2 %shard_map.30 = (f32[2,384,3072]{2,1,0:T(8,128)S(1)}, f32[8,128]{1,0:T(8,128)S(1)}) custom-call(bf16[2,1,384,3072]{3,2,1,0:T(8,128)(2,1)} %traces_ref.3), custom_call_target="tpu_custom_call" | custom-call | tf_op jit(solution)/shard_map/pallas_call | solution.py:526
  233.8 0.0 copy-done
  233.8 3.8 %shard_map.31 = (bf16[2,1,384,3072]{3,2,1,0:T(8,128)(2,1)}, bf16[2,1,384,3072]{3,2,1,0:T(8,128)(2,1)}) custom-call(f32[8,128]{1,0:T(8,128)S(1)} %get-tuple-element.4.fit_ref, bf16[2,1,384,3072]{3,2,1,0:T(8,128)(2,1)S(1)} %copy-done, f32[2,384,3072]{2,1,0:T(8,128)S(1)} %get-tuple-element.5.mult_ref), custom_call_target="tpu_custom_call" | custom-call | tf_op jit(solution)/shard_map/pallas_call | solution.py:555
Async XLA Ops:
  0.6 233.2 %copy-start = (bf16[2,1,384,3072]{3,2,1,0:T(8,128)(2,1)S(1)}, bf16[2,1,384,3072]{3,2,1,0:T(8,128)(2,1)}, u32[]{:S(2)}) copy-start(bf16[2,1,384,3072]{3,2,1,0:T(8,128)(2,1)} %traces_ref.3) | copy-start | bytes 14155780

commit v5 on v4

--- a/solution.py
+++ b/solution.py
@@ -101,7 +101,7 @@
 
 def line_kernel(
     chunks, kept, sizes, ready, schedule, freqs,
-    traces_ref, mult_ref, fit_ref,
+    traces_ref, mult_ref, fit_ref, mine_ref,
     grid, stage, acc, packed, partial_in,
     load_sem, piece_send, piece_recv, ici_recv, far_send, end_send, pair_send, pair_recv,
     result_send, result_recv, full_send, full_recv, sum_send, sum_recv,
@@ -282,6 +282,7 @@
         greet(across, shot)
         pl.semaphore_wait(barrier, 5)
 
+    again = pltpu.make_async_copy(traces_ref.at[:, 0], mine_ref, load_sem.at[3])
     load(0).wait()
     at_once = [d for d in range(len(schedule)) if sum(schedule[d][2:4]) <= early]
 
@@ -291,6 +292,7 @@
             piece(d).start()
         load(1).wait()
         load(2).wait()
+        again.start()
         for d in range(len(schedule)):
             if d not in at_once:
                 piece(d).start()
@@ -333,6 +335,7 @@
         give(0, (freq, mid * 2 + core)).wait_send()
         loop(half, chunks, lambda i: full(i).wait_recv())
         give_fit().wait_recv()
+        again.wait()
 
     @pl.when(jnp.logical_not(is_end))
     def _():
@@ -359,6 +362,7 @@
         loop(0, lead, lambda i: to_end(z, taken(i), 0).start())
         load(1).wait()
         load(2).wait()
+        again.start()
         for d in range(len(schedule)):
             if schedule[d][4] < 0:
                 piece(d).wait_recv()
@@ -435,6 +439,7 @@
         fit_im = jnp.broadcast_to(num_im / total_count / scaled_den, (1, LANES))
         fit_ref[...] = jnp.concatenate([fit_re, fit_im, jnp.zeros((6, LANES), jnp.float32)], axis=0)
         give_fit().start()
+        again.wait()
 
         def drain(i):
             to_far(z, sent(i), 0).wait_send()
@@ -465,7 +470,7 @@
 
 
 def epilogue_kernel(
-    strip, width, fit_ref, traces_ref, mult_ref, multiples_ref, primaries_ref,
+    strip, width, fit_ref, mine_ref, mult_ref, multiples_ref, primaries_ref,
     multiples, primaries, sems,
 ):
     rows, order = mult_ref.shape[1], mult_ref.shape[2]
@@ -493,8 +498,8 @@
             columns = pl.ds(q * width, width)
             mult_re = mult_ref[0, here(s), columns]
             mult_im = mult_ref[1, here(s), columns]
-            data_re = traces_ref[0, 0, here(s), columns].astype(jnp.float32)
-            data_im = traces_ref[1, 0, here(s), columns].astype(jnp.float32)
+            data_re = mine_ref[0, here(s), columns].astype(jnp.float32)
+            data_im = mine_ref[1, here(s), columns].astype(jnp.float32)
             prim_re = data_re - (fit_re * mult_re - fit_im * mult_im)
             prim_im = data_im - (fit_re * mult_im + fit_im * mult_re)
             primaries[0, here(s), columns] = prim_re.astype(jnp.bfloat16)
@@ -523,24 +528,22 @@
     schedule = end_schedule(chunks, sizes, ready)
     pieces = len(schedule)
     dma = pltpu.SemaphoreType.DMA
-    mult, fit = pl.pallas_call(
+    mult, fit, mine = pl.pallas_call(
         functools.partial(line_kernel, chunks, kept, sizes, ready, schedule, freqs),
         out_shape=(
             pltpu.VMEM((2, rows, order), jnp.float32),
             pltpu.VMEM((8, LANES), jnp.float32),
+            pltpu.VMEM((2, rows, order), jnp.bfloat16),
         ),
         in_specs=[pl.BlockSpec(memory_space=pltpu.HBM)],
-        out_specs=(
-            pl.BlockSpec(memory_space=pltpu.VMEM),
-            pl.BlockSpec(memory_space=pltpu.VMEM),
-        ),
+        out_specs=(pl.BlockSpec(memory_space=pltpu.VMEM),) * 3,
         scratch_shapes=[
             pltpu.VMEM((2, order, order), jnp.bfloat16),
             pltpu.VMEM((2, rows, (chunks - kept) * LANES), jnp.float32),
             pltpu.VMEM((24, LANES), jnp.float32),
             pltpu.VMEM((5, 8, LANES), jnp.float32),
             pltpu.VMEM((5, 8, LANES), jnp.float32),
-            dma((3,)), dma((pieces,)), dma((pieces,)), dma((3, chunks)), dma((2, chunks)),
+            dma((4,)), dma((pieces,)), dma((pieces,)), dma((3, chunks)), dma((2, chunks)),
             dma((3, chunks)), dma((4, chunks)), dma((4, chunks)),
             dma((groups, half)), dma((groups, half)), dma((half,)), dma((half,)), dma((6,)), dma((6,)),
         ],
@@ -563,7 +566,7 @@
             dma((2, rows // strip)),
         ],
         compiler_params=pltpu.CompilerParams(vmem_limit_bytes=24 * 1024 * 1024),
-    )(fit, traces, mult)
+    )(fit, mine, mult)
 
 
 def solution(mesh):

time: 238 us -> 238 us (level)
  no operation moved by 1% of the time
where the time goes in v5:
time: 238 us
  Pallas kernels  237 us (100%)
    pallas_call x1, Pallas kernels, on_a_line(): pl.pallas_call(functools.partial(line_kernel, chunks, kept, sizes, ready,...  233 us

profile of v5, /device:TPU:1, one launch (start us, length us, event | category | flops | bytes accessed | tf_op | source)
XLA Modules:
  0.0 237.5 jit_solution(16138568203228035501)
XLA Ops:
  0.6 233.0 %shard_map.30 = (f32[2,384,3072]{2,1,0:T(8,128)S(1)}, f32[8,128]{1,0:T(8,128)S(1)}, bf16[2,384,3072]{2,1,0:T(8,128)(2,1)S(1)}) custom-call(bf16[2,1,384,3072]{3,2,1,0:T(8,128)(2,1)} %traces_ref.1), custom_call_target="tpu_custom_call" | custom-call | tf_op jit(solution)/shard_map/pallas_call | solution.py:531
  233.7 3.8 %shard_map.31 = (bf16[2,1,384,3072]{3,2,1,0:T(8,128)(2,1)}, bf16[2,1,384,3072]{3,2,1,0:T(8,128)(2,1)}) custom-call(f32[8,128]{1,0:T(8,128)S(1)} %get-tuple-element.5.fit_ref, bf16[2,384,3072]{2,1,0:T(8,128)(2,1)S(1)} %get-tuple-element.6.mine_ref, f32[2,384,3072]{2,1,0:T(8,128)S(1)} %get-tuple-element.7.mult_ref), custom_call_target="tpu_custom_call" | custom-call | tf_op jit(solution)/shard_map/pallas_call | solution.py:558
